TPU v7x, 256 devices: a whole 4x4x8 slice. The times are simulated.
256 devices in a mesh: dp: 64 (over x, z, core), tensor: 4 (over y).
Axes of the slice: x: 4, y: 4, z: 8, core: 2. Of those that a mesh axis runs over, the one named last changes fastest.
Arguments:
- activations: bfloat16 [768, 8192], P('dp', 'tensor'), may hold values from -400 to 400, as said below
- weight: bfloat16 [8192, 28672], P('dp', 'tensor'), may hold values from -0.0625 to 0.0625
Outputs:
- channel_mean: float32 [8192], P('dp')
- column_errors: float32 [4, 28672], P(None, ('tensor', 'dp'))
- errors: float32 [4], replicated
Inputs may be any that keep to these rules, and one draw needn't show every extreme that they name: activations and weight are finite real values within the ranges stated above.
All inputs are finite; a program needn't handle non-finite values.
Results may differ from a plain program's by a relative error of at most 0.0012.
The roundings to bfloat16 on the way count: a program that leaves them out, or rounds other values in their place, can miss the bound.
Values may be sent and summed in bfloat16 or wider, within the bound.
A program may use at most 128 MiB of HBM per device.

v0:
```python
import functools
import math
import jax
import jax.numpy as jnp
from jax import lax
from jax.sharding import Mesh
from jax.sharding import PartitionSpec as P

D = 8192
F = 28672
GROUP = 128
GRID = 4
DP = ("dp_0", "dp_1", "dp_2")
DP_TENSOR = ("dp_0", "dp_1", "dp_2", "tensor")
TENSOR_DP = ("tensor", "dp_0", "dp_1", "dp_2")


def laid_out(parts, dim):
    parts = jnp.moveaxis(parts, 0, dim)
    dims = parts.shape
    return parts.reshape(*dims[:dim], dims[dim] * dims[dim + 1], *dims[dim + 2 :])


def from_everyone(shard, axis):
    devices = lax.axis_size(axis)
    return lax.all_to_all(
        jnp.broadcast_to(shard[None], (devices, *shard.shape)), axis, 0, 0, tiled=True
    )


def gather_directly(shard, axis, dim):
    return laid_out(from_everyone(shard, axis), dim)


def by_axis(shard, axes):
    return functools.reduce(lax.psum, axes, shard)


def soft_round(values):
    return values - jnp.sin(2.0 * math.pi * values) / (2.0 * math.pi)


def scale_table(channel_mean):
    ratios = jnp.arange(GRID, dtype=jnp.float32) / GRID
    raw = jnp.exp(ratios[:, None] * jnp.log(channel_mean)[None, :])
    top = jnp.max(raw, axis=1, keepdims=True)
    bottom = jnp.min(raw, axis=1, keepdims=True)
    return raw / jnp.sqrt(top * bottom)


def on_device(activations, weight):
    widened = gather_directly(activations, "tensor", 1)
    gathered = lax.all_gather(widened, DP, axis=0, tiled=True)
    columns = lax.all_to_all(weight, DP, split_axis=1, concat_axis=0, tiled=True)
    width = columns.shape[1]
    token_count = gathered.shape[0]
    channel_mean = jnp.sum(jnp.abs(gathered), axis=0, dtype=jnp.float32) / token_count + 1e-06
    scales = scale_table(channel_mean)
    base_out = jnp.dot(gathered, columns, preferred_element_type=jnp.float32)
    weight_float = columns.astype(jnp.float32)

    def local_error(factor):
        scaled = weight_float * factor[:, None]
        grouped = scaled.reshape(D // GROUP, GROUP, width)
        quant_step = (jnp.max(jnp.abs(grouped), axis=1, keepdims=True) + 1e-06) / 7.0
        levels = soft_round(grouped / quant_step)
        dequant = ((levels * quant_step).reshape(D, width) / factor[:, None]).astype(jnp.bfloat16)
        quant_out = jnp.dot(gathered, dequant, preferred_element_type=jnp.float32)
        residue = quant_out - base_out
        return jnp.sum(residue * residue, axis=0)

    column_sums = lax.map(local_error, scales)
    totals = by_axis(jnp.sum(column_sums, axis=1), DP_TENSOR)
    errors = totals / (token_count * F)
    column_errors = column_sums / token_count
    rows = D // lax.axis_size(DP)
    own_mean = lax.dynamic_slice_in_dim(channel_mean, lax.axis_index(DP) * rows, rows)
    return (own_mean, column_errors, errors)


def solution(mesh):
    torus = Mesh(
        mesh.devices.reshape(4, 8, 2, mesh.shape["tensor"]), ("dp_0", "dp_1", "dp_2", "tensor")
    )
    placed = (P(DP, "tensor"), P(DP, "tensor"))
    return jax.shard_map(
        on_device,
        mesh=torus,
        in_specs=placed,
        out_specs=(P(DP), P(None, TENSOR_DP), P()),
        check_vma=False,
    )
```

profile of v0, /device:TPU:2, one launch (start us, length us, event | category | flops | bytes accessed | tf_op | source)
XLA Modules:
  0.0 334.3 jit_solution(7435003003157472509)
XLA Ops:
  7.2 0.0 all-gather.3.cloned.1.call-start
  7.2 0.9 broadcast_in_dim.7
  8.1 10.9 %all_to_all.24 = bf16[4,12,2048]{2,1,0:T(8,128)(2,1)S(1)} all-to-all(bf16[4,12,2048]{2,1,0:T(8,128)(2,1)S(1)} %broadcast_in_dim.7), channel_id=1, replica_groups=mesh['dp_0'=4,'dp_1'=8,'dp_2'=2,'tensor'=4] {'tensor'}, dimensions={0} | all-to-all | bytes 393216 | tf_op jit(solution)/shard_map/all_to_all | solution.py:26
  19.0 0.2 copy.13
  19.2 0.8 reshape.54
  20.0 0.0 all-gather.3.cloned.1.call-update
  20.0 3.9 %copy.14 = bf16[128,7168]{0,1:T(8,128)(2,1)} copy(bf16[128,7168]{1,0:T(8,128)(2,1)} %param.5) | data formatting | bytes 3670016 | tf_op args[1]
  23.9 12.0 %all-to-all-start.1 = ((bf16[128,64,112]{0,2,1:T(8,128)(2,1)}), bf16[128,64,112]{0,2,1:T(8,128)(2,1)S(1)}, u32[]{:S(2)}, u32[]{:S(2)}) async-start(bf16[128,64,112]{0,2,1:T(8,128)(2,1)} %bitcast.7), calls=%async_computation.1 | async-start | bytes 3670016 | tf_op jit(solution)/shard_map/all_to_all | solution.py:54
  36.0 52.4 %all-to-all-done.1 = bf16[128,64,112]{0,2,1:T(8,128)(2,1)S(1)} async-done(((bf16[128,64,112]{0,2,1:T(8,128)(2,1)}), bf16[128,64,112]{0,2,1:T(8,128)(2,1)S(1)}, u32[]{:S(2)}, u32[]{:S(2)}) %all-to-all-start.1) | async-done | bytes 1835040 | tf_op jit(solution)/shard_map/all_to_all | solution.py:54
  88.4 2.1 bitcast_convert_fusion
  90.5 5.4 %copy.16 = f32[8192,112]{1,0:T(8,128)} copy(f32[8192,112]{0,1:T(8,128)} %bitcast_convert_fusion) | data formatting | bytes 7340032 | tf_op jit(solution)/shard_map/while | solution.py:72
  96.0 36.0 %all-gather.3.cloned.1.call-done = bf16[64,12,8192]{2,1,0:T(8,128)(2,1)} async-done(((bf16[1,12,8192]{2,1,0:T(8,128)(2,1)}), bf16[64,12,8192]{2,1,0:T(8,128)(2,1)}) %all-gather.3.cloned.1.call-update) | async-done | bytes 12582928 | tf_op jit(solution)/shard_map/all_gather | solution.py:53
  131.9 16.8 %reshape.55 = bf16[768,8192]{1,0:T(8,128)(2,1)} reshape(bf16[64,12,8192]{2,1,0:T(8,128)(2,1)} %all-gather.3.cloned.1.call-done) | data formatting | bytes 25165824
  148.8 7.6 %convert_reduce_fusion = f32[8192]{0:T(1024)S(1)} fusion(bf16[768,8192]{1,0:T(8,128)(2,1)} %reshape.55), kind=kLoop, calls=%fused_computation.11 | loop fusion | flops 18866176 | bytes 12615680 | tf_op jit(solution)/shard_map/reduce_sum | solution.py:57
  156.5 0.3 fusion.9
  156.7 0.1 fusion.8
  156.9 8.7 %fusion.5 = f32[768,112]{0,1:T(8,128)S(1)} fusion(bf16[768,8192]{1,0:T(8,128)(2,1)} %reshape.55, bf16[128,64,112]{0,2,1:T(8,128)(2,1)S(1)} %all-to-all-done.1), kind=kOutput, calls=%fused_computation.12 | convolution fusion | flops 1409286144 | bytes 14761984 | tf_op jit(solution)/shard_map/dot_general | solution.py:59
  165.6 122.5 %while.10 = (s32[]{:T(128)}, f32[4,112]{1,0:T(4,128)S(1)}, f32[4,8192]{1,0:T(4,128)S(1)}, f32[8192,112]{1,0:T(8,128)}, bf16[768,8192]{1,0:T(8,128)(2,1)}, /*index=5*/f32[768,112]{0,1:T(8,128)S(1)}, s32[]{:T(128)}, s32[]{:T(128)}) while((s32[]{:T(128)}, f32[4,112]{1,0:T(4,128)S(1)}, f32[4,8192]{1,0:T(4,128)S(1)}, f32[8192,112]{1,0:T(8,128)}, ...), condition=%wide.region_6.7_spmd, body=%wide.region_3.6_spmd.sunk | while | flops 1419643776 | bytes 38864320 | solution.py:72
  165.8 0.0 copy-start
  165.9 3.2 abs_reduce_fusion.2
  169.1 0.2 copy-done
  169.3 18.3 %fusion.24 = bf16[8192,112]{1,0:T(8,128)(2,1)S(1)} fusion(f32[8192,112]{1,0:T(8,128)S(1)} %copy-done, f32[64,112]{1,0:T(8,128)S(1)} %add_multiply_fusion.2, f32[8192]{0:T(1024)S(1)} %bitcast.55), kind=kLoop, calls=%fused_computation.3.clone.1 | loop fusion | flops 7340032 | bytes 5566464 | tf_op jit(solution)/shard_map/while/body/eval_jaxpr/convert_element_type | solution.py:67
  187.5 8.8 %fusion.25 = f32[112]{0:T(128)S(1)} fusion(f32[768,112]{0,1:T(8,128)S(1)} %get-tuple-element.130, bf16[8192,112]{1,0:T(8,128)(2,1)S(1)} %fusion.24, bf16[768,8192]{1,0:T(8,128)(2,1)} %get-tuple-element.129), kind=kOutput, calls=%fused_computation.8.clone.1 | convolution fusion | flops 1409544064 | bytes 14762432 | tf_op jit(solution)/shard_map/while/body/eval_jaxpr/dot_general | solution.py:68
  196.4 0.0 copy-start
  196.5 3.2 abs_reduce_fusion.2
  199.7 0.2 copy-done
  199.8 18.3 %fusion.24 = bf16[8192,112]{1,0:T(8,128)(2,1)S(1)} fusion(f32[8192,112]{1,0:T(8,128)S(1)} %copy-done, f32[64,112]{1,0:T(8,128)S(1)} %add_multiply_fusion.2, f32[8192]{0:T(1024)S(1)} %bitcast.55), kind=kLoop, calls=%fused_computation.3.clone.1 | loop fusion | flops 7340032 | bytes 5566464 | tf_op jit(solution)/shard_map/while/body/eval_jaxpr/convert_element_type | solution.py:67
  218.1 8.8 %fusion.25 = f32[112]{0:T(128)S(1)} fusion(f32[768,112]{0,1:T(8,128)S(1)} %get-tuple-element.130, bf16[8192,112]{1,0:T(8,128)(2,1)S(1)} %fusion.24, bf16[768,8192]{1,0:T(8,128)(2,1)} %get-tuple-element.129), kind=kOutput, calls=%fused_computation.8.clone.1 | convolution fusion | flops 1409544064 | bytes 14762432 | tf_op jit(solution)/shard_map/while/body/eval_jaxpr/dot_general | solution.py:68
  227.0 0.0 copy-start
  227.0 3.2 abs_reduce_fusion.2
  230.2 0.2 copy-done
  230.4 18.3 %fusion.24 = bf16[8192,112]{1,0:T(8,128)(2,1)S(1)} fusion(f32[8192,112]{1,0:T(8,128)S(1)} %copy-done, f32[64,112]{1,0:T(8,128)S(1)} %add_multiply_fusion.2, f32[8192]{0:T(1024)S(1)} %bitcast.55), kind=kLoop, calls=%fused_computation.3.clone.1 | loop fusion | flops 7340032 | bytes 5566464 | tf_op jit(solution)/shard_map/while/body/eval_jaxpr/convert_element_type | solution.py:67
  248.7 8.8 %fusion.25 = f32[112]{0:T(128)S(1)} fusion(f32[768,112]{0,1:T(8,128)S(1)} %get-tuple-element.130, bf16[8192,112]{1,0:T(8,128)(2,1)S(1)} %fusion.24, bf16[768,8192]{1,0:T(8,128)(2,1)} %get-tuple-element.129), kind=kOutput, calls=%fused_computation.8.clone.1 | convolution fusion | flops 1409544064 | bytes 14762432 | tf_op jit(solution)/shard_map/while/body/eval_jaxpr/dot_general | solution.py:68
  257.6 0.0 copy-start
  257.6 3.2 abs_reduce_fusion.2
  260.8 0.2 copy-done
  261.0 18.3 %fusion.24 = bf16[8192,112]{1,0:T(8,128)(2,1)S(1)} fusion(f32[8192,112]{1,0:T(8,128)S(1)} %copy-done, f32[64,112]{1,0:T(8,128)S(1)} %add_multiply_fusion.2, f32[8192]{0:T(1024)S(1)} %bitcast.55), kind=kLoop, calls=%fused_computation.3.clone.1 | loop fusion | flops 7340032 | bytes 5566464 | tf_op jit(solution)/shard_map/while/body/eval_jaxpr/convert_element_type | solution.py:67
  279.3 8.8 %fusion.25 = f32[112]{0:T(128)S(1)} fusion(f32[768,112]{0,1:T(8,128)S(1)} %get-tuple-element.130, bf16[8192,112]{1,0:T(8,128)(2,1)S(1)} %fusion.24, bf16[768,8192]{1,0:T(8,128)(2,1)} %get-tuple-element.129), kind=kOutput, calls=%fused_computation.8.clone.1 | convolution fusion | flops 1409544064 | bytes 14762432 | tf_op jit(solution)/shard_map/while/body/eval_jaxpr/dot_general | solution.py:68
  288.1 0.7 fusion.12
  288.8 9.1 %psum.28 = f32[4]{0:T(128)S(1)} all-reduce(f32[4]{0:T(128)S(1)} %get-tuple-element.70), channel_id=1, replica_groups=mesh['dp_0'=4,'dp_1'=8,'dp_2'=2,'tensor'=4] {'dp_0'}, use_global_device_ids=true, to_apply=%region_8.9 | all-reduce | flops 4 | bytes 32 | tf_op jit(solution)/shard_map/psum | solution.py:36
  298.0 15.8 %psum.29 = f32[4]{0:T(128)S(1)} all-reduce(f32[4]{0:T(128)S(1)} %psum.28), channel_id=1, replica_groups=mesh['dp_0'=4,'dp_1'=8,'dp_2'=2,'tensor'=4] {'dp_1'}, use_global_device_ids=true, to_apply=%region_9.10 | all-reduce | flops 4 | bytes 32 | tf_op jit(solution)/shard_map/psum | solution.py:36
  313.7 2.5 psum.30
  316.2 10.2 %psum.31 = f32[4]{0:T(128)S(1)} all-reduce(f32[4]{0:T(128)S(1)} %psum.30), channel_id=1, replica_groups=mesh['dp_0'=4,'dp_1'=8,'dp_2'=2,'tensor'=4] {'tensor'}, use_global_device_ids=true, to_apply=%region_11.12 | all-reduce | flops 4 | bytes 32 | tf_op jit(solution)/shard_map/psum | solution.py:36
  326.3 0.5 broadcast_multiply_fusion.1
  326.9 0.6 dynamic_slice.7
  (16 shorter events, 0.4 us)
Async XLA Ops:
  7.2 124.8 %all-gather.3.cloned.1.call-start = ((), (), s32[]{:S(2)}) async-start(), calls=%async_computation.2 | async-start | bytes 17039360 | tf_op jit(solution)/shard_map/all_gather | solution.py:53
  23.9 64.5 %all-to-all-start.1 = ((bf16[128,64,112]{0,2,1:T(8,128)(2,1)}), bf16[128,64,112]{0,2,1:T(8,128)(2,1)S(1)}, u32[]{:S(2)}, u32[]{:S(2)}) async-start(bf16[128,64,112]{0,2,1:T(8,128)(2,1)} %bitcast.7), calls=%async_computation.1 | async-start | bytes 3670016 | tf_op jit(solution)/shard_map/all_to_all | solution.py:54
  165.8 3.5 %copy-start = (f32[8192,112]{1,0:T(8,128)S(1)}, f32[8192,112]{1,0:T(8,128)}, u32[]{:S(2)}) copy-start(f32[8192,112]{1,0:T(8,128)} %get-tuple-element.128) | copy-start | bytes 11010052 | tf_op jit(solution)/shard_map/while
  196.4 3.5 %copy-start = (f32[8192,112]{1,0:T(8,128)S(1)}, f32[8192,112]{1,0:T(8,128)}, u32[]{:S(2)}) copy-start(f32[8192,112]{1,0:T(8,128)} %get-tuple-element.128) | copy-start | bytes 11010052 | tf_op jit(solution)/shard_map/while
  227.0 3.5 %copy-start = (f32[8192,112]{1,0:T(8,128)S(1)}, f32[8192,112]{1,0:T(8,128)}, u32[]{:S(2)}) copy-start(f32[8192,112]{1,0:T(8,128)} %get-tuple-element.128) | copy-start | bytes 11010052 | tf_op jit(solution)/shard_map/while
  257.6 3.5 %copy-start = (f32[8192,112]{1,0:T(8,128)S(1)}, f32[8192,112]{1,0:T(8,128)}, u32[]{:S(2)}) copy-start(f32[8192,112]{1,0:T(8,128)} %get-tuple-element.128) | copy-start | bytes 11010052 | tf_op jit(solution)/shard_map/while
Sparse Core Ops, SparseCore 0:
  20.1 111.7 all-gather.2
where the time goes:
time: 335 us; the launch traced here: 334 us
  other arithmetic  97.2 us (29%)
  waiting for transfers between devices  88.4 us (26%)
  blocking collectives  48.5 us (14%)
  matrix products  44 us (13%)
  local copies, waits for them, and re-layouts  29.7 us (9%)
  between operations  14.1 us (4%)
  starting transfers between devices  12.1 us (4%)
    convert_element_type x4, other arithmetic, local_error(): ((levels * quant_step).reshape(D, width) / factor[:, None]).astype(jnp.bf...  73 us
    all_to_all x1, waiting for transfers between devices, on_device(): lax.all_to_all(weight, DP, split_axis=1, concat_axis=0, tiled=True)  52.4 us
    psum x4, blocking collectives, by_axis(): return functools.reduce(lax.psum, axes, shard)  37.5 us
    all_gather x1, waiting for transfers between devices, on_device(): gathered = lax.all_gather(widened, DP, axis=0, tiled=True)  36 us
    dot_general x4, matrix products, local_error(): quant_out = jnp.dot(gathered, dequant, preferred_element_type=jnp.float32)  35.2 us
    unnamed x3, local copies, waits for them, and re-layouts  21.6 us
    reduce_max x4, other arithmetic, local_error(): jnp.max(jnp.abs(grouped), axis=1, keepdims=True) + 1e-06  12.7 us
    all_to_all x1, starting transfers between devices, on_device(): lax.all_to_all(weight, DP, split_axis=1, concat_axis=0, tiled=True)  12 us
  transfers between devices with their start and end apart: 2, of which 2 were waited for; matrix products, arithmetic and copies ran while one was open for 3% of the time, Pallas kernels for 0%

commit v1 on v0

--- a/solution.py
+++ b/solution.py
@@ -50,7 +50,10 @@
 
 def on_device(activations, weight):
     widened = gather_directly(activations, "tensor", 1)
-    gathered = lax.all_gather(widened, DP, axis=0, tiled=True)
+    peers = lax.axis_size(DP)
+    blocks = jnp.stack([widened for _ in range(peers)])
+    blocks = lax.all_to_all(blocks, DP, split_axis=0, concat_axis=0)
+    gathered = jnp.concatenate(blocks, axis=0)
     columns = lax.all_to_all(weight, DP, split_axis=1, concat_axis=0, tiled=True)
     width = columns.shape[1]
     token_count = gathered.shape[0]

time: 335 us -> 642 us (1.92)
  waiting for transfers between devices: 88.4 us -> 404 us
  blocking collectives: 48.5 us -> 33.9 us
  between operations: 14.1 us -> 0.73 us
  starting transfers between devices: 12.1 us -> 24.1 us
  local copies, waits for them, and re-layouts: 29.7 us -> 36.3 us
    all_to_all x0 -> x2, waiting for transfers between devices: none -> 360 us  [the longest x1 358 us: on_device(): blocks = lax.all_to_all(blocks, DP, split_axis=0, concat_axis=0)]
    all_gather x1 -> x0, waiting for transfers between devices: 36 us -> none  [on_device(): gathered = lax.all_gather(widened, DP, axis=0, tiled=True)]
    unnamed x3, local copies, waits for them, and re-layouts: 21.6 us -> 4.16 us
    reshape x0 -> x1, local copies, waits for them, and re-layouts: none -> 16.9 us  [on_device(): gathered = jnp.concatenate(blocks, axis=0)]
    all_to_all x0 -> x2, starting transfers between devices: none -> 12.1 us  [the longest x1 7.64 us: on_device(): blocks = lax.all_to_all(blocks, DP, split_axis=0, concat_axis=0)]
    all_to_all x1 -> x0, blocking collectives: 10.9 us -> none  [from_everyone(): lax.all_to_all(jnp.broadcast_to(shard[None], (devices, *shard.shape)), ax...]
    all_to_all x1, waiting for transfers between devices: 52.4 us -> 43.5 us  [on_device(): lax.all_to_all(weight, DP, split_axis=1, concat_axis=0, tiled=True)]
  transfers between devices with their start and end apart: 2 -> 3, of which waited for: 2 -> 3; matrix products, arithmetic and copies ran while one was open for 3% -> 2% of each run, Pallas kernels for 0% -> 0%
where the time goes in v1:
time: 642 us; the launch traced here: 639 us
  waiting for transfers between devices  404 us (63%)
  other arithmetic  96.3 us (15%)
  matrix products  44 us (7%)
  local copies, waits for them, and re-layouts  36.3 us (6%)
  blocking collectives  33.9 us (5%)
  starting transfers between devices  24.1 us (4%)
    all_to_all x1, waiting for transfers between devices, on_device(): blocks = lax.all_to_all(blocks, DP, split_axis=0, concat_axis=0)  358 us
    convert_element_type x4, other arithmetic, local_error(): ((levels * quant_step).reshape(D, width) / factor[:, None]).astype(jnp.bf...  73 us
    all_to_all x1, waiting for transfers between devices, on_device(): lax.all_to_all(weight, DP, split_axis=1, concat_axis=0, tiled=True)  43.5 us
    dot_general x4, matrix products, local_error(): quant_out = jnp.dot(gathered, dequant, preferred_element_type=jnp.float32)  35.2 us
    psum x4, blocking collectives, by_axis(): return functools.reduce(lax.psum, axes, shard)  33.9 us
    reshape x1, local copies, waits for them, and re-layouts, on_device(): gathered = jnp.concatenate(blocks, axis=0)  16.9 us
  transfers between devices with their start and end apart: 3, of which 3 were waited for; matrix products, arithmetic and copies ran while one was open for 2% of the time, Pallas kernels for 0%

profile of v1, /device:TPU:2, one launch (start us, length us, event | category | flops | bytes accessed | tf_op | source)
XLA Modules:
  0.0 639.5 jit_solution(4678732688074810310)
XLA Ops:
  0.6 1.6 broadcast_in_dim.7
  2.2 4.5 all-to-all-start
  6.7 3.9 copy.14
  10.6 2.8 all-to-all-done
  13.3 12.0 %all-to-all-start.2 = ((bf16[128,64,112]{0,2,1:T(8,128)(2,1)}), bf16[128,64,112]{0,2,1:T(8,128)(2,1)S(1)}, u32[]{:S(2)}, u32[]{:S(2)}) async-start(bf16[128,64,112]{0,2,1:T(8,128)(2,1)} %bitcast.7), calls=%async_computation.2 | async-start | bytes 3670016 | tf_op jit(solution)/shard_map/all_to_all | solution.py:57
  25.4 0.2 copy.13
  25.5 0.1 pad
  25.6 0.2 copy.18
  25.8 43.5 %all-to-all-done.2 = bf16[128,64,112]{0,2,1:T(8,128)(2,1)S(1)} async-done(((bf16[128,64,112]{0,2,1:T(8,128)(2,1)}), bf16[128,64,112]{0,2,1:T(8,128)(2,1)S(1)}, u32[]{:S(2)}, u32[]{:S(2)}) %all-to-all-start.2) | async-done | bytes 1835040 | tf_op jit(solution)/shard_map/all_to_all | solution.py:57
  69.3 5.9 stack.3
  75.2 7.6 %all-to-all-start.1 = ((bf16[64,12,8192]{2,1,0:T(8,128)(2,1)}), bf16[64,12,8192]{2,1,0:T(8,128)(2,1)}, u32[]{:S(2)}, u32[]{:S(2)}) async-start(bf16[64,12,8192]{2,1,0:T(8,128)(2,1)} %stack.3), calls=%async_computation.1 | async-start | bytes 33554432 | tf_op jit(solution)/shard_map/all_to_all | solution.py:55
  82.9 2.1 bitcast_convert_fusion
  85.0 5.4 copy.16
  90.4 357.6 %all-to-all-done.1 = bf16[64,12,8192]{2,1,0:T(8,128)(2,1)} async-done(((bf16[64,12,8192]{2,1,0:T(8,128)(2,1)}), bf16[64,12,8192]{2,1,0:T(8,128)(2,1)}, u32[]{:S(2)}, u32[]{:S(2)}) %all-to-all-start.1) | async-done | bytes 12582944 | tf_op jit(solution)/shard_map/all_to_all | solution.py:55
  448.0 7.4 %convert_reduce_fusion = f32[8192]{0:T(1024)S(1)} fusion(bf16[64,12,8192]{2,1,0:T(8,128)(2,1)} %all-to-all-done.1), kind=kLoop, calls=%fused_computation.11 | loop fusion | flops 18866176 | bytes 12615680 | tf_op jit(solution)/shard_map/reduce_sum | solution.py:60
  455.4 0.3 fusion.9
  455.7 0.1 fusion.8
  455.8 16.9 %reshape.55 = bf16[768,8192]{1,0:T(8,128)(2,1)} reshape(bf16[64,12,8192]{2,1,0:T(8,128)(2,1)} %all-to-all-done.1) | data formatting | bytes 25165824 | tf_op jit(solution)/shard_map/reshape | solution.py:56
  472.7 8.7 %fusion.5 = f32[768,112]{0,1:T(8,128)S(1)} fusion(bf16[768,8192]{1,0:T(8,128)(2,1)} %reshape.55, bf16[128,64,112]{0,2,1:T(8,128)(2,1)S(1)} %all-to-all-done.2), kind=kOutput, calls=%fused_computation.12 | convolution fusion | flops 1409286144 | bytes 14761984 | tf_op jit(solution)/shard_map/dot_general | solution.py:62
  481.4 122.3 %while.10 = (s32[]{:T(128)}, f32[4,112]{1,0:T(4,128)S(1)}, f32[4,8192]{1,0:T(4,128)S(1)}, f32[8192,112]{1,0:T(8,128)}, bf16[768,8192]{1,0:T(8,128)(2,1)}, /*index=5*/f32[768,112]{0,1:T(8,128)S(1)}, s32[]{:T(128)}, s32[]{:T(128)}) while((s32[]{:T(128)}, f32[4,112]{1,0:T(4,128)S(1)}, f32[4,8192]{1,0:T(4,128)S(1)}, f32[8192,112]{1,0:T(8,128)}, ...), condition=%wide.region_6.7_spmd, body=%wide.region_3.6_spmd.sunk | while | flops 1419643776 | bytes 38864312 | solution.py:75
  481.4 0.0 copy-start
  481.5 3.0 abs_reduce_fusion.2
  484.5 0.3 copy-done
  484.9 18.3 %fusion.24 = bf16[8192,112]{1,0:T(8,128)(2,1)S(1)} fusion(f32[8192,112]{1,0:T(8,128)S(1)} %copy-done, f32[64,112]{1,0:T(8,128)S(1)} %add_multiply_fusion.2, f32[8192]{0:T(1024)S(1)} %bitcast.58), kind=kLoop, calls=%fused_computation.3.clone.1 | loop fusion | flops 7340032 | bytes 5566464 | tf_op jit(solution)/shard_map/while/body/eval_jaxpr/convert_element_type | solution.py:70
  503.1 8.8 %fusion.25 = f32[112]{0:T(128)S(1)} fusion(f32[768,112]{0,1:T(8,128)S(1)} %get-tuple-element.130, bf16[8192,112]{1,0:T(8,128)(2,1)S(1)} %fusion.24, bf16[768,8192]{1,0:T(8,128)(2,1)} %get-tuple-element.129), kind=kOutput, calls=%fused_computation.8.clone.1 | convolution fusion | flops 1409544064 | bytes 14762432 | tf_op jit(solution)/shard_map/while/body/eval_jaxpr/dot_general | solution.py:71
  512.0 0.0 copy-start
  512.0 3.0 abs_reduce_fusion.2
  515.1 0.3 copy-done
  515.4 18.3 %fusion.24 = bf16[8192,112]{1,0:T(8,128)(2,1)S(1)} fusion(f32[8192,112]{1,0:T(8,128)S(1)} %copy-done, f32[64,112]{1,0:T(8,128)S(1)} %add_multiply_fusion.2, f32[8192]{0:T(1024)S(1)} %bitcast.58), kind=kLoop, calls=%fused_computation.3.clone.1 | loop fusion | flops 7340032 | bytes 5566464 | tf_op jit(solution)/shard_map/while/body/eval_jaxpr/convert_element_type | solution.py:70
  533.7 8.8 %fusion.25 = f32[112]{0:T(128)S(1)} fusion(f32[768,112]{0,1:T(8,128)S(1)} %get-tuple-element.130, bf16[8192,112]{1,0:T(8,128)(2,1)S(1)} %fusion.24, bf16[768,8192]{1,0:T(8,128)(2,1)} %get-tuple-element.129), kind=kOutput, calls=%fused_computation.8.clone.1 | convolution fusion | flops 1409544064 | bytes 14762432 | tf_op jit(solution)/shard_map/while/body/eval_jaxpr/dot_general | solution.py:71
  542.6 0.0 copy-start
  542.6 3.0 abs_reduce_fusion.2
  545.7 0.3 copy-done
  546.0 18.3 %fusion.24 = bf16[8192,112]{1,0:T(8,128)(2,1)S(1)} fusion(f32[8192,112]{1,0:T(8,128)S(1)} %copy-done, f32[64,112]{1,0:T(8,128)S(1)} %add_multiply_fusion.2, f32[8192]{0:T(1024)S(1)} %bitcast.58), kind=kLoop, calls=%fused_computation.3.clone.1 | loop fusion | flops 7340032 | bytes 5566464 | tf_op jit(solution)/shard_map/while/body/eval_jaxpr/convert_element_type | solution.py:70
  564.3 8.8 %fusion.25 = f32[112]{0:T(128)S(1)} fusion(f32[768,112]{0,1:T(8,128)S(1)} %get-tuple-element.130, bf16[8192,112]{1,0:T(8,128)(2,1)S(1)} %fusion.24, bf16[768,8192]{1,0:T(8,128)(2,1)} %get-tuple-element.129), kind=kOutput, calls=%fused_computation.8.clone.1 | convolution fusion | flops 1409544064 | bytes 14762432 | tf_op jit(solution)/shard_map/while/body/eval_jaxpr/dot_general | solution.py:71
  573.1 0.0 copy-start
  573.2 3.0 abs_reduce_fusion.2
  576.3 0.3 copy-done
  576.6 18.3 %fusion.24 = bf16[8192,112]{1,0:T(8,128)(2,1)S(1)} fusion(f32[8192,112]{1,0:T(8,128)S(1)} %copy-done, f32[64,112]{1,0:T(8,128)S(1)} %add_multiply_fusion.2, f32[8192]{0:T(1024)S(1)} %bitcast.58), kind=kLoop, calls=%fused_computation.3.clone.1 | loop fusion | flops 7340032 | bytes 5566464 | tf_op jit(solution)/shard_map/while/body/eval_jaxpr/convert_element_type | solution.py:70
  594.9 8.8 %fusion.25 = f32[112]{0:T(128)S(1)} fusion(f32[768,112]{0,1:T(8,128)S(1)} %get-tuple-element.130, bf16[8192,112]{1,0:T(8,128)(2,1)S(1)} %fusion.24, bf16[768,8192]{1,0:T(8,128)(2,1)} %get-tuple-element.129), kind=kOutput, calls=%fused_computation.8.clone.1 | convolution fusion | flops 1409544064 | bytes 14762432 | tf_op jit(solution)/shard_map/while/body/eval_jaxpr/dot_general | solution.py:71
  603.7 0.7 fusion.12
  604.4 7.8 %psum.28 = f32[4]{0:T(128)S(1)} all-reduce(f32[4]{0:T(128)S(1)} %get-tuple-element.70), channel_id=1, replica_groups=mesh['dp_0'=4,'dp_1'=8,'dp_2'=2,'tensor'=4] {'dp_0'}, use_global_device_ids=true, to_apply=%region_8.9 | all-reduce | flops 4 | bytes 32 | tf_op jit(solution)/shard_map/psum | solution.py:36
  612.2 14.8 %psum.29 = f32[4]{0:T(128)S(1)} all-reduce(f32[4]{0:T(128)S(1)} %psum.28), channel_id=1, replica_groups=mesh['dp_0'=4,'dp_1'=8,'dp_2'=2,'tensor'=4] {'dp_1'}, use_global_device_ids=true, to_apply=%region_9.10 | all-reduce | flops 4 | bytes 32 | tf_op jit(solution)/shard_map/psum | solution.py:36
  627.0 2.5 psum.30
  629.5 8.9 %psum.31 = f32[4]{0:T(128)S(1)} all-reduce(f32[4]{0:T(128)S(1)} %psum.30), channel_id=1, replica_groups=mesh['dp_0'=4,'dp_1'=8,'dp_2'=2,'tensor'=4] {'tensor'}, use_global_device_ids=true, to_apply=%region_11.12 | all-reduce | flops 4 | bytes 32 | tf_op jit(solution)/shard_map/psum | solution.py:36
  638.4 0.5 broadcast_multiply_fusion.1
  638.9 0.6 dynamic_slice.7
  (16 shorter events, 0.4 us)
Async XLA Ops:
  2.2 11.1 %all-to-all-start = ((bf16[4,12,2048]{2,1,0:T(8,128)(2,1)}), bf16[4,12,2048]{2,1,0:T(8,128)(2,1)S(1)}, u32[]{:S(2)}, u32[]{:S(2)}) async-start(bf16[4,12,2048]{2,1,0:T(8,128)(2,1)} %broadcast_in_dim.7), calls=%async_computation | async-start | bytes 524288 | tf_op jit(solution)/shard_map/all_to_all | solution.py:26
  13.3 56.0 %all-to-all-start.2 = ((bf16[128,64,112]{0,2,1:T(8,128)(2,1)}), bf16[128,64,112]{0,2,1:T(8,128)(2,1)S(1)}, u32[]{:S(2)}, u32[]{:S(2)}) async-start(bf16[128,64,112]{0,2,1:T(8,128)(2,1)} %bitcast.7), calls=%async_computation.2 | async-start | bytes 3670016 | tf_op jit(solution)/shard_map/all_to_all | solution.py:57
  75.2 372.8 %all-to-all-start.1 = ((bf16[64,12,8192]{2,1,0:T(8,128)(2,1)}), bf16[64,12,8192]{2,1,0:T(8,128)(2,1)}, u32[]{:S(2)}, u32[]{:S(2)}) async-start(bf16[64,12,8192]{2,1,0:T(8,128)(2,1)} %stack.3), calls=%async_computation.1 | async-start | bytes 33554432 | tf_op jit(solution)/shard_map/all_to_all | solution.py:55
  481.4 3.5 copy-start
  512.0 3.5 copy-start
  542.6 3.5 copy-start
  573.1 3.5 copy-start
